TPU v7x, 32 devices: a whole 2x2x4 slice. The times are simulated.
32 devices in a mesh: row: 8 (over z, core), col: 4 (over y, x).
Axes of the slice: x: 2, y: 2, z: 4, core: 2. Of those that a mesh axis runs over, the one named last changes fastest.
Arguments:
- pair_exchange: bfloat16 [64, 16, 1024], P(('row', 'col')), may hold values from -6 to 6
- conduction: bfloat16 [64, 4, 1024], P(('row', 'col')), may hold values from -6 to 6
- valence: bfloat16 [64, 4, 1024], P(('row', 'col')), may hold values from -6 to 6
- coulomb: float32 [1024], replicated, may hold values from 0.5 to 5
- screening: float32 [34, 1024], replicated, may hold values from 0.1 to 1
- energies: float32 [64, 16], P(('row', 'col')), may hold values from 1 to 9
- vectors: bfloat16 [64, 512], P(('row', 'col')), may hold values from -6 to 6
- k_coords: int32 [64, 2], P(('row', 'col')), may hold values from 0 to 31, as said below
Outputs:
- residual_block: float32 [64, 512], P(('row', 'col'))
- alpha: float32 [32, 32], replicated
Inputs may be any that keep to these rules, and one draw needn't show every extreme that they name: `k_coords`: each row holds a k-point's coordinates on the periodic 32 x 2 mesh, first then second; every mesh point occurs exactly once.
All inputs are finite; a program needn't handle non-finite values.
Results may differ from a plain program's by a relative error of at most 0.0028.
Values may be sent and summed in bfloat16 or wider, within the bound.
A program may use at most 64 MiB of HBM per device.

v0:
```python
import jax
import jax.numpy as jnp
from jax import lax
from jax.sharding import PartitionSpec as P

MX = 32
highest = lax.Precision.HIGHEST


def pair_factors(conduction, valence):
    count, valence_count, plane_count = valence.shape
    joined = (
        valence.astype(jnp.float32)[:, :, None, :] * conduction.astype(jnp.float32)[:, None, :, :]
    )
    return joined.reshape(count, valence_count * conduction.shape[1], plane_count).astype(
        jnp.bfloat16
    )


def transfer_index(rows_at, cols_at, mesh_cols):
    delta_first = jnp.mod(rows_at[:, None, 0] - cols_at[None, :, 0], MX)
    delta_second = jnp.mod(rows_at[:, None, 1] - cols_at[None, :, 1], mesh_cols)
    fold_first = jnp.minimum(delta_first, MX - delta_first)
    fold_second = jnp.minimum(delta_second, mesh_cols - delta_second)
    return (fold_first * (mesh_cols // 2 + 1) + fold_second).astype(jnp.int32)


def on_device(pair_exchange, conduction, valence, coulomb, screening, energies, vectors, k_coords):
    local_count, band_count, plane_count = pair_exchange.shape
    vector_count = vectors.shape[1] // band_count
    row_count = lax.axis_size("row")
    col_count = lax.axis_size("col")
    total_count = local_count * row_count * col_count
    mesh_cols = total_count // MX
    moving = vectors.reshape(local_count, band_count, vector_count)
    partial_density = jnp.einsum(
        "ktg,ktn->gn", pair_exchange, moving, preferred_element_type=jnp.float32
    )
    density = lax.psum(partial_density, ("row", "col"))
    block_size = 128
    sweeps = plane_count // block_size
    col_cond, col_val, col_vec, col_at = (
        lax.all_gather(conduction, "row", axis=0, tiled=True),
        lax.all_gather(valence, "row", axis=0, tiled=True),
        lax.all_gather(vectors, "row", axis=0, tiled=True),
        lax.all_gather(k_coords, "row", axis=0, tiled=True),
    )
    row_cond, row_val, row_at = (
        lax.all_gather(conduction, "col", axis=0, tiled=True),
        lax.all_gather(valence, "col", axis=0, tiled=True),
        lax.all_gather(k_coords, "col", axis=0, tiled=True),
    )
    row_pairs = pair_factors(row_cond, row_val)
    col_pairs = pair_factors(col_cond, col_val)
    indices = transfer_index(row_at, col_at, mesh_cols)
    col_moving = col_vec.reshape(-1, band_count, vector_count)

    def square_sweep(sweep_index, running):
        anchor = sweep_index * block_size
        coupling = jnp.take(
            lax.dynamic_slice_in_dim(screening, anchor, block_size, 1), indices, axis=0
        )
        row_block = lax.dynamic_slice_in_dim(row_pairs, anchor, block_size, 2)
        col_block = lax.dynamic_slice_in_dim(col_pairs, anchor, block_size, 2)
        col_proj = jnp.einsum(
            "ktg,ktn->kng", col_block, col_moving, preferred_element_type=jnp.float32
        )
        potential = jnp.einsum("ijg,jng->ing", coupling, col_proj, precision=highest)
        return running + jnp.einsum(
            "ktg,kng->ktn", row_block.astype(jnp.float32), potential, precision=highest
        )

    forward = lax.fori_loop(
        0,
        sweeps,
        square_sweep,
        jnp.zeros((row_pairs.shape[0], band_count, vector_count), jnp.float32),
    )
    owned = lax.psum_scatter(
        forward.reshape(col_count, local_count, band_count, vector_count),
        "col",
        scatter_dimension=0,
        tiled=True,
    )[0]
    moving_wide = moving.astype(jnp.float32)
    exchange_term = jnp.einsum(
        "ktg,gn->ktn", pair_exchange.astype(jnp.float32) * coulomb, density, precision=highest
    )
    applied = (
        energies[:, :, None] * moving_wide
        + 2.0 / (total_count * band_count) * exchange_term
        - owned / total_count
    )
    gram = jnp.einsum("ktm,ktn->mn", moving_wide, applied, precision=highest)
    alpha = lax.psum(gram, ("row", "col")) / (total_count * band_count)
    residual = applied - jnp.einsum("ktm,mn->ktn", moving_wide, alpha, precision=highest)
    return (residual.reshape(local_count, band_count * vector_count), alpha)


def solution(mesh):
    in_specs = (
        P(("row", "col"), None, None),
        P(("row", "col"), None, None),
        P(("row", "col"), None, None),
        P(),
        P(),
        P(("row", "col"), None),
        P(("row", "col"), None),
        P(("row", "col"), None),
    )
    out_specs = (P(("row", "col"), None), P())
    return jax.shard_map(
        on_device, mesh=mesh, in_specs=in_specs, out_specs=out_specs, check_vma=False
    )
```

profile of v0, /device:TPU:0, one launch (start us, length us, event | category | flops | bytes accessed | tf_op | source)
XLA Modules:
  0.0 299.9 jit_solution(13418184121838847277)
XLA Ops:
  8.7 13.5 %all-gather.2 = s32[8,2,2]{2,1,0:T(2,128)S(1)} all-gather(s32[1,2,2]{2,1,0:T(2,128)S(1)} %bitcast.65), channel_id=1, replica_groups=mesh['row'=8,'col'=4] {'row'}, dimensions={0}, use_global_device_ids=true | all-gather | bytes 144 | tf_op jit(solution)/shard_map/all_gather | solution.py:46
  22.1 8.1 %all-gather.1 = s32[4,2,2]{2,1,0:T(2,128)S(1)} all-gather(s32[1,2,2]{2,1,0:T(2,128)S(1)} %bitcast.66), channel_id=1, replica_groups=mesh['row'=8,'col'=4] {'col'}, dimensions={0}, use_global_device_ids=true | all-gather | bytes 80 | tf_op jit(solution)/shard_map/all_gather | solution.py:51
  30.2 14.3 %all_gather.23 = bf16[16,4,1024]{2,1,0:T(4,128)(2,1)S(1)} all-gather(bf16[2,4,1024]{2,1,0:T(4,128)(2,1)} %param.12), channel_id=1, replica_groups=mesh['row'=8,'col'=4] {'row'}, dimensions={0}, use_global_device_ids=true | all-gather | bytes 147456 | tf_op jit(solution)/shard_map/all_gather | solution.py:44
  44.5 8.3 %all_gather.21 = bf16[8,4,1024]{2,1,0:T(4,128)(2,1)S(1)} all-gather(bf16[2,4,1024]{2,1,0:T(4,128)(2,1)S(1)} %copy-done.2), channel_id=1, replica_groups=mesh['row'=8,'col'=4] {'col'}, dimensions={0}, use_global_device_ids=true | all-gather | bytes 81920 | tf_op jit(solution)/shard_map/all_gather | solution.py:50
  52.9 14.0 %all_gather.24 = bf16[16,4,1024]{2,1,0:T(4,128)(2,1)S(1)} all-gather(bf16[2,4,1024]{2,1,0:T(4,128)(2,1)S(1)} %copy-done.3), channel_id=1, replica_groups=mesh['row'=8,'col'=4] {'row'}, dimensions={0}, use_global_device_ids=true | all-gather | bytes 147456 | tf_op jit(solution)/shard_map/all_gather | solution.py:43
  66.9 7.2 %all_gather.22 = bf16[8,4,1024]{2,1,0:T(4,128)(2,1)S(1)} all-gather(bf16[2,4,1024]{2,1,0:T(4,128)(2,1)S(1)} %copy-done.3), channel_id=1, replica_groups=mesh['row'=8,'col'=4] {'col'}, dimensions={0}, use_global_device_ids=true | all-gather | bytes 81920 | tf_op jit(solution)/shard_map/all_gather | solution.py:49
  75.8 12.8 %all-gather = bf16[8,2,512]{2,1,0:T(2,128)(2,1)S(1)} all-gather(bf16[1,2,512]{2,1,0:T(2,128)(2,1)S(1)} %bitcast.64), channel_id=1, replica_groups=mesh['row'=8,'col'=4] {'row'}, dimensions={0}, use_global_device_ids=true | all-gather | bytes 18432 | tf_op jit(solution)/shard_map/all_gather | solution.py:45
  88.7 33.2 %while.14 = (s32[]{:T(128)}, f32[8,16,32]{2,1,0:T(8,128)S(1)}, bf16[8,16,1024]{2,1,0:T(8,128)(2,1)S(1)}, bf16[16,16,1024]{2,1,0:T(8,128)(2,1)S(1)}, bf16[16,16,3...) while((s32[]{:T(128)}, f32[8,16,32]{2,1,0:T(8,128)S(1)}, ...), condition=%wide.region_2.3_spmd.clone, body=%wide.region_1.2_spmd.clone.sunk | while | flops 14714503 | bytes 2319689 | solution.py:73
  88.7 0.7 constant_dynamic-slice_fusion.2
  91.4 1.1 convolution_bitcast_fusion.8
  92.9 0.7 constant_dynamic-slice_fusion.2
  95.5 1.1 convolution_bitcast_fusion.8
  99.7 1.1 convolution_bitcast_fusion.8
  103.8 1.1 convolution_bitcast_fusion.8
  108.0 1.1 convolution_bitcast_fusion.8
  112.1 1.1 convolution_bitcast_fusion.8
  116.3 1.1 convolution_bitcast_fusion.8
  117.8 0.7 constant_dynamic-slice_fusion.2
  120.4 1.1 convolution_bitcast_fusion.8
  122.8 0.9 convolution_bitcast_fusion.2
  123.7 20.8 %reduce-scatter.4.cloned.1.call-done = f32[1,2,16,32]{3,2,1,0:T(8,128)} async-done(((f32[4,2,16,32]{3,2,1,0:T(8,128)}), f32[1,2,16,32]{3,2,1,0:T(8,128)}) %reduce-scatter.4.cloned.1.call-update) | async-done | bytes 4112
  144.5 105.8 %all-reduce.3.cloned.1.call-done = f32[1024,32]{0,1:T(8,128)} async-done(((f32[1024,32]{0,1:T(8,128)}), f32[1024,32]{0,1:T(8,128)}) %all-reduce.3.cloned.1.call-update) | async-done | bytes 131088 | tf_op jit(solution)/shard_map/psum | solution.py:39
  250.3 1.1 fusion.17
  251.7 39.3 %psum.15 = f32[32,32]{0,1:T(8,128)S(1)} all-reduce(f32[32,32]{0,1:T(8,128)S(1)} %convolution_bitcast_fusion.4), channel_id=1, replica_groups=mesh['row'=8,'col'=4] {'row','col'}, use_global_device_ids=true, to_apply=%region_4.5 | all-reduce | flops 1024 | bytes 8192 | tf_op jit(solution)/shard_map/psum | solution.py:95
  (119 shorter events, 26.9 us)
Async XLA Ops:
  8.0 0.7 copy-start.6
  8.0 136.5 %reduce-scatter.4.cloned.1.call-start = ((), (), s32[]{:S(2)}) async-start(), calls=%async_computation.2 | async-start | bytes 81920
  30.2 14.3 %copy-start.2 = (bf16[2,4,1024]{2,1,0:T(4,128)(2,1)S(1)}, bf16[2,4,1024]{2,1,0:T(4,128)(2,1)}, u32[]{:S(2)}) copy-start(bf16[2,4,1024]{2,1,0:T(4,128)(2,1)} %param.12) | copy-start | bytes 49156
  44.5 8.3 %copy-start.3 = (bf16[2,4,1024]{2,1,0:T(4,128)(2,1)S(1)}, bf16[2,4,1024]{2,1,0:T(4,128)(2,1)}, u32[]{:S(2)}) copy-start(bf16[2,4,1024]{2,1,0:T(4,128)(2,1)} %param.11) | copy-start | bytes 49156
  75.2 0.7 copy-start.4
  121.9 0.6 copy-start
  121.9 0.9 copy-start.1
  122.6 127.7 %all-reduce.3.cloned.1.call-start = ((), (), s32[]{:S(2)}) async-start(), calls=%async_computation.1 | async-start | bytes 262144 | tf_op jit(solution)/shard_map/psum | solution.py:39
  123.7 126.6 %copy-start.5 = (f32[1024]{0:T(1024)S(1)}, f32[1024]{0:T(1024)}, u32[]{:S(2)}) copy-start(f32[1024]{0:T(1024)} %param.13) | copy-start | bytes 12292
  123.7 126.7 %copy-start.7 = (f32[2,16]{1,0:T(2,128)S(1)}, f32[2,16]{1,0:T(2,128)}, u32[]{:S(2)}) copy-start(f32[2,16]{1,0:T(2,128)} %param.15) | copy-start | bytes 388
Sparse Core Ops, SparseCore 0:
  122.7 21.7 reduce-scatter.3
Sparse Core Ops, SparseCore 1:
  128.6 121.7 all-reduce.2
where the time goes:
time: 301 us; the launch traced here: 300 us
  waiting for transfers between devices  127 us (42%)
  blocking collectives  117 us (39%)
  local copies, waits for them, and re-layouts  21.7 us (7%)
  matrix products  16.1 us (5%)
  between operations  15.6 us (5%)
    psum x1, waiting for transfers between devices, on_device(): density = lax.psum(partial_density, ('row', 'col'))  106 us
    psum x1, blocking collectives, on_device(): alpha = lax.psum(gram, ('row', 'col')) / (total_count * band_count)  39.3 us
    unnamed x3, waiting for transfers between devices  20.8 us
    all_gather x1, blocking collectives, on_device(): lax.all_gather(valence, 'row', axis=0, tiled=True)  14.3 us
    all_gather x1, blocking collectives, on_device(): lax.all_gather(conduction, 'row', axis=0, tiled=True)  14 us
    all_gather x1, blocking collectives, on_device(): lax.all_gather(k_coords, 'row', axis=0, tiled=True)  13.5 us
    all_gather x1, blocking collectives, on_device(): lax.all_gather(vectors, 'row', axis=0, tiled=True)  12.8 us
    dot_general x8, matrix products, square_sweep(): jnp.einsum('ijg,jng->ing', coupling, col_proj, precision=highest)  8.7 us
  transfers between devices with their start and end apart: 2, of which 2 were waited for; matrix products, arithmetic and copies ran while one was open for 0% of the time, Pallas kernels for 0%

commit v1 on v0

--- a/solution.py
+++ b/solution.py
@@ -5,6 +5,12 @@
 
 MX = 32
 highest = lax.Precision.HIGHEST
+
+
+def summed_here(value, name):
+    shards = lax.all_gather(value, name, axis=0, tiled=False)
+    total = shards.sum(axis=0)
+    return total
 
 
 def pair_factors(conduction, valence):
@@ -92,7 +98,7 @@
         - owned / total_count
     )
     gram = jnp.einsum("ktm,ktn->mn", moving_wide, applied, precision=highest)
-    alpha = lax.psum(gram, ("row", "col")) / (total_count * band_count)
+    alpha = summed_here(gram, ("row", "col")) / (total_count * band_count)
     residual = applied - jnp.einsum("ktm,mn->ktn", moving_wide, alpha, precision=highest)
     return (residual.reshape(local_count, band_count * vector_count), alpha)
 

time: 301 us -> 330 us (1.096)
  blocking collectives: 117 us -> 146 us
    all_gather x0 -> x1, blocking collectives: none -> 68 us  [summed_here(): shards = lax.all_gather(value, name, axis=0, tiled=False)]
    psum x1 -> x0, blocking collectives: 39.3 us -> none  [on_device(): alpha = lax.psum(gram, ('row', 'col')) / (total_count * band_count)]
where the time goes in v1:
time: 330 us; the launch traced here: 329 us
  blocking collectives  146 us (44%)
  waiting for transfers between devices  127 us (38%)
  local copies, waits for them, and re-layouts  21.9 us (7%)
  matrix products  16.1 us (5%)
  between operations  15.6 us (5%)
    psum x1, waiting for transfers between devices, on_device(): density = lax.psum(partial_density, ('row', 'col'))  106 us
    all_gather x1, blocking collectives, summed_here(): shards = lax.all_gather(value, name, axis=0, tiled=False)  68 us
    unnamed x3, waiting for transfers between devices  20.8 us
    all_gather x1, blocking collectives, on_device(): lax.all_gather(valence, 'row', axis=0, tiled=True)  14.3 us
    all_gather x1, blocking collectives, on_device(): lax.all_gather(conduction, 'row', axis=0, tiled=True)  14 us
    all_gather x1, blocking collectives, on_device(): lax.all_gather(k_coords, 'row', axis=0, tiled=True)  13.5 us
    all_gather x1, blocking collectives, on_device(): lax.all_gather(vectors, 'row', axis=0, tiled=True)  12.8 us
    dot_general x8, matrix products, square_sweep(): jnp.einsum('ijg,jng->ing', coupling, col_proj, precision=highest)  8.7 us
  transfers between devices with their start and end apart: 2, of which 2 were waited for; matrix products, arithmetic and copies ran while one was open for 0% of the time, Pallas kernels for 0%

profile of v1, /device:TPU:0, one launch (start us, length us, event | category | flops | bytes accessed | tf_op | source)
XLA Modules:
  0.0 328.8 jit_solution(13574463554490786483)
XLA Ops:
  8.7 13.5 %all-gather.3 = s32[8,2,2]{2,1,0:T(2,128)S(1)} all-gather(s32[1,2,2]{2,1,0:T(2,128)S(1)} %bitcast.67), channel_id=1, replica_groups=mesh['row'=8,'col'=4] {'row'}, dimensions={0}, use_global_device_ids=true | all-gather | bytes 144 | tf_op jit(solution)/shard_map/all_gather | solution.py:52
  22.1 8.1 %all-gather.2 = s32[4,2,2]{2,1,0:T(2,128)S(1)} all-gather(s32[1,2,2]{2,1,0:T(2,128)S(1)} %bitcast.68), channel_id=1, replica_groups=mesh['row'=8,'col'=4] {'col'}, dimensions={0}, use_global_device_ids=true | all-gather | bytes 80 | tf_op jit(solution)/shard_map/all_gather | solution.py:57
  30.2 14.3 %all_gather.29 = bf16[16,4,1024]{2,1,0:T(4,128)(2,1)S(1)} all-gather(bf16[2,4,1024]{2,1,0:T(4,128)(2,1)} %param.12), channel_id=1, replica_groups=mesh['row'=8,'col'=4] {'row'}, dimensions={0}, use_global_device_ids=true | all-gather | bytes 147456 | tf_op jit(solution)/shard_map/all_gather | solution.py:50
  44.5 8.3 %all_gather.27 = bf16[8,4,1024]{2,1,0:T(4,128)(2,1)S(1)} all-gather(bf16[2,4,1024]{2,1,0:T(4,128)(2,1)S(1)} %copy-done.2), channel_id=1, replica_groups=mesh['row'=8,'col'=4] {'col'}, dimensions={0}, use_global_device_ids=true | all-gather | bytes 81920 | tf_op jit(solution)/shard_map/all_gather | solution.py:56
  52.9 14.0 %all_gather.30 = bf16[16,4,1024]{2,1,0:T(4,128)(2,1)S(1)} all-gather(bf16[2,4,1024]{2,1,0:T(4,128)(2,1)S(1)} %copy-done.3), channel_id=1, replica_groups=mesh['row'=8,'col'=4] {'row'}, dimensions={0}, use_global_device_ids=true | all-gather | bytes 147456 | tf_op jit(solution)/shard_map/all_gather | solution.py:49
  66.9 7.2 %all_gather.28 = bf16[8,4,1024]{2,1,0:T(4,128)(2,1)S(1)} all-gather(bf16[2,4,1024]{2,1,0:T(4,128)(2,1)S(1)} %copy-done.3), channel_id=1, replica_groups=mesh['row'=8,'col'=4] {'col'}, dimensions={0}, use_global_device_ids=true | all-gather | bytes 81920 | tf_op jit(solution)/shard_map/all_gather | solution.py:55
  75.8 12.8 %all-gather.1 = bf16[8,2,512]{2,1,0:T(2,128)(2,1)S(1)} all-gather(bf16[1,2,512]{2,1,0:T(2,128)(2,1)S(1)} %bitcast.66), channel_id=1, replica_groups=mesh['row'=8,'col'=4] {'row'}, dimensions={0}, use_global_device_ids=true | all-gather | bytes 18432 | tf_op jit(solution)/shard_map/all_gather | solution.py:51
  88.7 33.2 %while.14 = (s32[]{:T(128)}, f32[8,16,32]{2,1,0:T(8,128)S(1)}, bf16[8,16,1024]{2,1,0:T(8,128)(2,1)S(1)}, bf16[16,16,1024]{2,1,0:T(8,128)(2,1)S(1)}, bf16[16,16,3...) while((s32[]{:T(128)}, f32[8,16,32]{2,1,0:T(8,128)S(1)}, ...), condition=%wide.region_2.3_spmd.clone, body=%wide.region_1.2_spmd.clone.sunk | while | flops 14714503 | bytes 2319689 | solution.py:79
  88.7 0.7 constant_dynamic-slice_fusion.2
  91.4 1.1 convolution_bitcast_fusion.8
  92.9 0.7 constant_dynamic-slice_fusion.2
  95.5 1.1 convolution_bitcast_fusion.8
  97.0 0.7 constant_dynamic-slice_fusion.2
  99.7 1.1 convolution_bitcast_fusion.8
  103.8 1.1 convolution_bitcast_fusion.8
  108.0 1.1 convolution_bitcast_fusion.8
  112.1 1.1 convolution_bitcast_fusion.8
  116.3 1.1 convolution_bitcast_fusion.8
  120.4 1.1 convolution_bitcast_fusion.8
  122.8 0.9 convolution_bitcast_fusion.2
  123.7 20.8 %reduce-scatter.4.cloned.1.call-done = f32[1,2,16,32]{3,2,1,0:T(8,128)} async-done(((f32[4,2,16,32]{3,2,1,0:T(8,128)}), f32[1,2,16,32]{3,2,1,0:T(8,128)}) %reduce-scatter.4.cloned.1.call-update) | async-done | bytes 4112
  144.5 105.8 %all-reduce.3.cloned.1.call-done = f32[1024,32]{0,1:T(8,128)} async-done(((f32[1024,32]{0,1:T(8,128)}), f32[1024,32]{0,1:T(8,128)}) %all-reduce.3.cloned.1.call-update) | async-done | bytes 131088 | tf_op jit(solution)/shard_map/psum | solution.py:45
  250.3 1.1 fusion.17
  251.7 68.0 %all-gather = f32[1024,32]{1,0:T(8,128)S(1)} all-gather(f32[32,32]{1,0:T(8,128)S(1)} %copy.19), channel_id=2, replica_groups=mesh['row'=8,'col'=4] {'row','col'}, dimensions={0}, use_global_device_ids=true | all-gather | bytes 135168 | tf_op jit(solution)/shard_map/all_gather | solution.py:11
  (122 shorter events, 27.1 us)
Async XLA Ops:
  8.0 0.7 copy-start.6
  8.0 136.5 %reduce-scatter.4.cloned.1.call-start = ((), (), s32[]{:S(2)}) async-start(), calls=%async_computation.2 | async-start | bytes 81920
  30.2 14.3 %copy-start.2 = (bf16[2,4,1024]{2,1,0:T(4,128)(2,1)S(1)}, bf16[2,4,1024]{2,1,0:T(4,128)(2,1)}, u32[]{:S(2)}) copy-start(bf16[2,4,1024]{2,1,0:T(4,128)(2,1)} %param.12) | copy-start | bytes 49156
  44.5 8.3 %copy-start.3 = (bf16[2,4,1024]{2,1,0:T(4,128)(2,1)S(1)}, bf16[2,4,1024]{2,1,0:T(4,128)(2,1)}, u32[]{:S(2)}) copy-start(bf16[2,4,1024]{2,1,0:T(4,128)(2,1)} %param.11) | copy-start | bytes 49156
  75.2 0.7 copy-start.4
  121.9 0.6 copy-start
  121.9 0.9 copy-start.1
  122.6 127.7 %all-reduce.3.cloned.1.call-start = ((), (), s32[]{:S(2)}) async-start(), calls=%async_computation.1 | async-start | bytes 262144 | tf_op jit(solution)/shard_map/psum | solution.py:45
  123.7 126.6 %copy-start.5 = (f32[1024]{0:T(1024)S(1)}, f32[1024]{0:T(1024)}, u32[]{:S(2)}) copy-start(f32[1024]{0:T(1024)} %param.13) | copy-start | bytes 12292
  123.7 126.6 %copy-start.7 = (f32[2,16]{1,0:T(2,128)S(1)}, f32[2,16]{1,0:T(2,128)}, u32[]{:S(2)}) copy-start(f32[2,16]{1,0:T(2,128)} %param.15) | copy-start | bytes 388
Sparse Core Ops, SparseCore 0:
  122.7 21.7 reduce-scatter.3
Sparse Core Ops, SparseCore 1:
  128.6 121.6 all-reduce.2
